TPU v7x, 256 devices: a whole 4x4x8 slice. The times are simulated.
256 devices in a mesh: seq: 16 (over z, x_lo), img: 8 (over y, x_hi), fsdp: 2 (over core).
Axes of the slice: x: 4 (x_hi: 2, x_lo: 2; x = x_hi * 2 + x_lo), y: 4, z: 8, core: 2. Of those that a mesh axis runs over, the one named last changes fastest.
Arguments:
- vision_feats: bfloat16 [8, 2304, 1024], P('img', ('seq', 'fsdp')), may hold values from -6 to 6
- ln_gain: float32 [1024], replicated, may hold values from 0.5 to 1.5
- ln_bias: float32 [1024], replicated, may hold values from -3 to 3
- w_in: bfloat16 [1024, 4096], P('fsdp', 'seq'), may hold values from -0.1875 to 0.1875
- b_in: float32 [4096], P('seq'), may hold values from -3 to 3
- w_out: bfloat16 [4096, 4096], P('seq', 'fsdp'), may hold values from -0.09375 to 0.09375
- lm_grad: bfloat16 [8, 4096, 4096], P('img', 'seq', 'fsdp'), may hold values from -0.079589844 to 0.079589844
- image_counts: int32 [8, 2], P('img'), may hold values from 1 to 3, as said below
- token_pos: int32 [8, 2304], P('img'), may hold values from 0 to 2047, as said below
Outputs:
- w_in_grad: float32 [1024, 4096], P(('img', 'fsdp'), 'seq')
- b_in_grad: float32 [4096], replicated
- w_out_grad: float32 [4096, 4096], P(('seq', 'img'), 'fsdp')
- b_out_grad: float32 [4096], replicated
- ln_gain_grad: float32 [1024], replicated
- ln_bias_grad: float32 [1024], replicated
Inputs may be any that keep to these rules, and one draw needn't show every extreme that they name: `image_counts`: in each group the 2 samples hold 4 images together, each sample one or more. `token_pos`: each image's 576 tokens take consecutive positions of its sample's sequence in order; a sample's images come in order without intersection, and images are numbered sample by sample as image_counts gives.
All inputs are finite; a program needn't handle non-finite values.
Results may differ from a plain program's by a relative error of at most 0.0047.
Values may be sent and summed in bfloat16 or wider, within the bound.
No kernel may reach another device: no remote copies, remote signals or barrier semaphores. Data moves between devices by JAX's collectives and lax.ppermute only.
A program may use at most 128 MiB of HBM per device.

v0:
```python
import jax
import jax.numpy as jnp
from jax import lax
from jax.sharding import Mesh
from jax.sharding import PartitionSpec as P

PATCH = 576
LEN = 2048
SEQ = ("seq_0", "seq_1")
IMG = ("img_0", "img_1")
SEQ_FSDP = ("seq_0", "seq_1", "fsdp")
SEQ_IMG_FSDP = ("seq_0", "seq_1", "img_0", "img_1", "fsdp")
IMG_FSDP = ("img_0", "img_1", "fsdp")
SEQ_IMG = ("seq_0", "seq_1", "img_0", "img_1")


def copy_for_each(array, axis):
    copies = jnp.broadcast_to(array, (lax.axis_size(axis), *array.shape))
    return lax.all_to_all(copies, axis, split_axis=0, concat_axis=0, tiled=True)


def in_order(pieces, dim):
    shape = list(pieces.shape[1:])
    shape[dim] *= pieces.shape[0]
    return jnp.moveaxis(pieces, 0, dim).reshape(shape)


def gather_directly(array, axis, dim):
    pieces = copy_for_each(array, axis)
    return in_order(pieces, dim)


def whole_of(array, axes, dim):
    if not axes:
        return array
    nearer = lax.all_gather(array, axes[-1], axis=dim, tiled=True)
    return whole_of(nearer, axes[:-1], dim)


def taken_together(array, axis):
    return copy_for_each(array, axis).sum(axis=0)


def in_blocks(array, dim, devices):
    shape = array.shape
    pieces = array.reshape(*shape[:dim], devices, shape[dim] // devices, *shape[dim + 1 :])
    return jnp.moveaxis(pieces, dim, 0)


def one_scatter(arrays, axis, dims):
    devices = lax.axis_size(axis)
    pieces = [in_blocks(a, dim, devices) for a, dim in zip(arrays, dims)]
    lines = jnp.concatenate([b.reshape(devices, -1) for b in pieces], axis=1)
    width = max(16, -(-lines.shape[1] // 1024) * 8)
    lines = jnp.pad(lines, ((0, 0), (0, width * 128 - lines.shape[1]))).reshape(-1, 128)
    vector, at, gathered = (lax.psum_scatter(lines, axis, tiled=True).reshape(-1), 0, [])
    for b in pieces:
        part = b[0]
        gathered.append(vector[at : at + part.size].reshape(part.shape))
        at += part.size
    return tuple(gathered)


def one_axis_at_a_time(array, axes):
    for axis in axes:
        array = lax.psum(array, axis)
    return array


def gelu_parts(preact):
    cumul = 0.5 * (1.0 + lax.erf(preact * 0.7071067811865476))
    density = jnp.exp(-0.5 * preact * preact) * 0.3989422804014327
    return (preact * cumul, cumul + preact * density)


def contract(left, right, left_dim, right_dim):
    return lax.dot_general(
        left, right, (((left_dim,), (right_dim,)), ((), ())), preferred_element_type=jnp.float32
    )


def own_columns(matrix, img_count, fsdp_count, fsdp_index):
    rows = matrix.shape[0]
    block = matrix.shape[1] // (img_count * fsdp_count)
    shaped = matrix.reshape(rows, img_count, fsdp_count, block)
    taken = lax.dynamic_index_in_dim(shaped, fsdp_index, axis=2, keepdims=False)
    return taken.reshape(rows, img_count * block)


def place_columns(vector, img_count, fsdp_count, fsdp_index):
    block = vector.shape[0] // img_count
    holder = jnp.zeros((img_count, fsdp_count, block), jnp.float32)
    holder = lax.dynamic_update_slice(
        holder, vector.reshape(img_count, 1, block), (0, fsdp_index, 0)
    )
    return holder.reshape(img_count * fsdp_count * block)


def per_device(vision_feats, ln_gain, ln_bias, w_in, b_in, w_out, lm_grad, image_counts, token_pos):
    seq_count = lax.axis_size(SEQ)
    seq_index = lax.axis_index(SEQ)
    img_count = lax.axis_size(IMG)
    fsdp_count = lax.axis_size("fsdp")
    fsdp_index = lax.axis_index("fsdp")
    lm_block = lm_grad[0]
    block_rows = lm_block.shape[0]
    half_width = lm_block.shape[1]
    position_count = block_rows * seq_count
    counts = image_counts[0]
    positions = token_pos[0]
    row_count = positions.shape[0]
    image_index = jnp.arange(row_count, dtype=jnp.int32) // PATCH
    bounds = jnp.cumsum(counts)
    sample = jnp.sum((image_index[:, None] >= bounds[None, :]).astype(jnp.int32), axis=1)
    abs_pos = sample * LEN + positions
    marker = jnp.zeros((position_count,), jnp.float32).at[abs_pos].set(1.0)
    own_mask = lax.dynamic_slice_in_dim(marker, seq_index * block_rows, block_rows).astype(
        jnp.bfloat16
    )
    out_bias_half = jnp.dot(own_mask[None, :], lm_block, preferred_element_type=jnp.float32)[0]
    out_bias_full = lax.dynamic_update_slice_in_dim(
        jnp.zeros((half_width * fsdp_count,), jnp.float32),
        out_bias_half,
        fsdp_index * half_width,
        0,
    )
    w_in_full = gather_directly(w_in, "fsdp", 0)
    gathered = lax.all_gather(vision_feats[0], SEQ_FSDP, axis=0, tiled=True)
    values = gathered.astype(jnp.float32)
    row_mean = jnp.mean(values, axis=1, keepdims=True)
    centred = values - row_mean
    row_var = jnp.mean(centred * centred, axis=1, keepdims=True)
    normed = centred * lax.rsqrt(row_var + 1e-05)
    normed_in = (normed * ln_gain + ln_bias).astype(jnp.bfloat16)
    preact = jnp.dot(normed_in, w_in_full, preferred_element_type=jnp.float32) + b_in
    activ, slope = gelu_parts(preact)
    hidden = activ.astype(jnp.bfloat16)
    hidden_width = hidden.shape[1]
    whole_grad = whole_of(lm_block, SEQ, 0)
    picked = whole_grad[abs_pos]
    hidden_part = contract(picked, w_out, 1, 1)
    w_out_part = contract(hidden, picked, 0, 0)
    hidden_grad = taken_together(hidden_part, "fsdp")
    preact_grad = (hidden_grad * slope).astype(jnp.bfloat16)
    own_normed_in = own_columns(normed_in, img_count, fsdp_count, fsdp_index)
    own_normed = own_columns(normed, img_count, fsdp_count, fsdp_index)
    own_w_in = own_columns(w_in_full.T, img_count, fsdp_count, fsdp_index)
    w_in_part = contract(own_normed_in, preact_grad, 0, 0)
    half_rows = row_count // fsdp_count
    own_rows = lax.dynamic_slice_in_dim(preact_grad, fsdp_index * half_rows, half_rows, 0)
    b_in_part = jnp.sum(own_rows, axis=0, dtype=jnp.float32)
    normed_grad = contract(preact_grad, own_w_in, 1, 0)
    gain_part = place_columns(
        jnp.sum(normed_grad * own_normed, axis=0), img_count, fsdp_count, fsdp_index
    )
    bias_part = place_columns(jnp.sum(normed_grad, axis=0), img_count, fsdp_count, fsdp_index)
    w_in_grad, w_out_grad = one_scatter((w_in_part, w_out_part), IMG, (0, 0))
    hidden_full = lax.dynamic_update_slice_in_dim(
        jnp.zeros((hidden_width * seq_count,), jnp.float32), b_in_part, seq_index * hidden_width, 0
    )
    gain_grad, bias_grad, b_in_grad, b_out_grad = (
        one_axis_at_a_time(gain_part, SEQ_IMG_FSDP),
        one_axis_at_a_time(bias_part, SEQ_IMG_FSDP),
        one_axis_at_a_time(hidden_full, SEQ_IMG_FSDP),
        one_axis_at_a_time(out_bias_full, SEQ_IMG_FSDP),
    )
    return (w_in_grad, b_in_grad, w_out_grad, b_out_grad, gain_grad, bias_grad)


def solution(mesh):
    finer = Mesh(
        mesh.devices.reshape(8, 2, 4, 2, mesh.shape["fsdp"]),
        ("seq_0", "seq_1", "img_0", "img_1", "fsdp"),
    )
    placed = (
        P(IMG, SEQ_FSDP, None),
        P(),
        P(),
        P("fsdp", SEQ),
        P(SEQ),
        P(SEQ, "fsdp"),
        P(IMG, SEQ, "fsdp"),
        P(IMG, None),
        P(IMG, None),
    )
    return jax.shard_map(
        per_device,
        mesh=finer,
        in_specs=placed,
        out_specs=(P(IMG_FSDP, SEQ), P(), P(SEQ_IMG, "fsdp"), P(), P(), P()),
        check_vma=False,
    )
```

profile of v0, /device:TPU:1, one launch (start us, length us, event | category | flops | bytes accessed | tf_op | source)
XLA Modules:
  0.0 471.8 jit_solution(9273449355537463096)
XLA Ops:
  7.3 0.7 all-gather.9.cloned.1.call-update
  8.0 0.7 all-gather.7.cloned.1.call-update
  8.7 42.9 %all-gather.9.cloned.1.call-done = bf16[1,512,2048]{2,1,0:T(8,128)(2,1)} async-done(((bf16[1,256,2048]{2,1,0:T(8,128)(2,1)}), bf16[1,512,2048]{2,1,0:T(8,128)(2,1)}) %all-gather.9.cloned.1.call-update) | async-done | bytes 2097168 | tf_op jit(solution)/shard_map/all_gather | solution.py:36
  51.7 0.2 reduce-window.8
  51.9 0.1 fusion.13
  52.0 70.0 %all-gather.7.cloned.1.call-done = bf16[1,2304,1024]{2,1,0:T(8,128)(2,1)} async-done(((bf16[1,72,1024]{2,1,0:T(8,128)(2,1)}), bf16[1,2304,1024]{2,1,0:T(8,128)(2,1)}) %all-gather.7.cloned.1.call-update) | async-done | bytes 4718608 | tf_op jit(solution)/shard_map/all_gather | solution.py:128
  122.1 6.8 %copy.20 = bf16[1,2304,1024]{1,2,0:T(8,128)(2,1)} copy(bf16[1,2304,1024]{2,1,0:T(8,128)(2,1)} %all-gather.7.cloned.1.call-done) | data formatting | bytes 9437184 | tf_op jit(solution)/shard_map/all_gather | solution.py:128
  128.9 3.2 convert_reduce_fusion
  132.1 0.6 copy-done.2
  132.6 1.3 fusion.3
  133.9 4.8 %fusion.1 = (f32[2304,1024]{0,1:T(8,128)}, bf16[2304,1024]{0,1:T(8,128)(2,1)S(1)}) fusion(bf16[1,2304,1024]{1,2,0:T(8,128)(2,1)S(1)} %copy-done.2, f32[2304]{0:T(1024)S(1)} %add_rsqrt_fusion, f32[2304]{0:T(1024)S(1)} %broadcast_multiply_fusion.1, f32[1024]{0:T(1024)S(1)} %copy-done.10, f32[1024]{0:T(1024)S(1)} %copy-done.11), kind=kLoop, calls=%fused_computation.5 | loop fusion | flops 14155776 | bytes 18900992 | tf_op jit(solution)/shard_map/mul | solution.py:133
  138.7 2.1 copy-done.3
  140.9 1.6 constant_dynamic-slice_fusion.2
  142.5 153.5 %all-gather.11.cloned.1.call-done = bf16[1,4096,2048]{2,1,0:T(8,128)(2,1)} async-done(((bf16[1,512,2048]{2,1,0:T(8,128)(2,1)}), bf16[1,4096,2048]{2,1,0:T(8,128)(2,1)}) %all-gather.11.cloned.1.call-update) | async-done | bytes 16777232 | tf_op jit(solution)/shard_map/all_gather | solution.py:36
  296.0 26.2 %gather_fusion = bf16[2304,2048]{1,0:T(8,128)(2,1)} fusion(bf16[4096,2048]{1,0:T(8,128)(2,1)} %bitcast.43, s32[3072]{0:T(1024)S(1)} %pad_clamp_fusion), kind=kCustom, calls=%fused_computation | custom fusion | bytes 18883584 | tf_op jit(solution)/shard_map/gather | solution.py:140
  322.2 5.2 %fusion.21 = f32[2304,256]{1,0:T(8,128)S(1)} fusion(bf16[2304,2048]{1,0:T(8,128)(2,1)} %gather_fusion, bf16[256,2048]{1,0:T(8,128)(2,1)S(1)} %copy-done), kind=kOutput, calls=%fused_computation.48 | convolution fusion | flops 2415919104 | bytes 12845056 | tf_op jit(solution)/shard_map/dot_general | solution.py:77
  327.5 0.3 broadcast_in_dim.6
  327.8 9.2 %all_to_all.10 = f32[2,2304,256]{2,1,0:T(8,128)} all-to-all(f32[2,2304,256]{2,1,0:T(8,128)S(1)} %broadcast_in_dim.6), channel_id=1, replica_groups=mesh['seq_0'=8,'seq_1'=2,'img_0'=4,'img_1'=2,'fsdp'=2] {'fsdp'}, dimensions={0} | all-to-all | bytes 9437184 | tf_op jit(solution)/shard_map/all_to_all | solution.py:19
  337.0 0.8 broadcast_in_dim.7
  337.9 3.8 all-to-all-start.1
  341.7 4.5 reduce_sum.66
  346.2 6.7 %fusion.9 = (bf16[2304,256]{1,0:T(8,128)(2,1)}, f32[2304,256]{1,0:T(8,128)S(1)}) fusion(f32[2304,256]{1,0:T(8,128)} %reduce_sum.66, f32[256]{0:T(256)S(1)} %copy-done.12, bf16[2304,1024]{0,1:T(8,128)(2,1)} %copy-done.3, bf16[1024,256]{1,0:T(8,128)(2,1)S(1)} %bitcast.50), kind=kOutput, calls=%fused_computation.18 | convolution fusion | flops 1214447616 | bytes 11142144 | tf_op jit(solution)/shard_map/dot_general | solution.py:135
  352.9 4.0 fusion.10
  356.9 2.0 reshape_reshape.7
  358.9 2.8 fusion.22
  361.7 0.1 reshape_reshape.6
  361.8 1.7 pad_maximum_fusion
  363.5 3.6 reshape.151
  367.1 9.0 %scatter_custom_fusion = f32[4096]{0:T(1024)S(1)} fusion(s32[2304]{0:T(1024)S(1)} %fusion.17, f32[2304]{0:T(1024)S(1)} %broadcast.81, f32[]{:T(128)} %constant.22.clone.1), kind=kCustom, calls=%fused_computation.39 | custom fusion | bytes 16388 | tf_op jit(solution)/shard_map/scatter | solution.py:116
  376.1 0.1 dynamic_slice.28
  376.2 0.2 fusion.11
  376.5 0.2 dynamic_update_slice.13
  376.7 5.0 %constant_dynamic-slice_fusion = f32[2304,8,1,64]{0,3,2,1:T(8,128)} fusion(f32[2304,8,2,64]{0,3,2,1:T(8,128)} %bitcast.46, s32[]{:T(128)S(6)} %select_n.40), kind=kLoop, calls=%fused_computation.44 | loop fusion | bytes 9437188 | tf_op jit(solution)/shard_map/jit(dynamic_index_in_dim)/dynamic_slice | solution.py:86
  381.8 6.2 %copy.21 = f32[2304,512]{1,0:T(8,128)} copy(f32[2304,512]{0,1:T(8,128)} %bitcast.47) | data formatting | bytes 9437184 | tf_op jit(solution)/shard_map/reshape | solution.py:87
  388.0 3.3 fusion.20
  391.3 0.1 reshape.158
  391.5 0.1 reshape.160
  391.7 0.2 convert_reduce_fusion.1
  391.9 0.3 dynamic_update_slice.12
  392.2 23.3 %all-reduce = (f32[4096]{0:T(1024)S(1)}, f32[4096]{0:T(1024)S(1)}, f32[1024]{0:T(1024)S(1)}, f32[1024]{0:T(1024)S(1)}) all-reduce(f32[4096]{0:T(1024)S(1)} %dynamic_update_slice.12, f32[4096]{0:T(1024)S(1)} %dynamic_update_slice.13, ...), channel_id=1, replica_groups=mesh['seq_0'=8,'seq_1'=2,'img_0'=4,'img_1'=2,'fsdp'=2] {'seq_0'}, use_global_device_ids=true, to_apply=%region_7.8 | all-reduce | flops 10240 | bytes 81920 | tf_op jit(solution)/shard_map/psum | solution.py:66
  415.5 5.9 %all-reduce.4 = (f32[4096]{0:T(1024)S(1)}, f32[4096]{0:T(1024)S(1)}, f32[1024]{0:T(1024)S(1)}, f32[1024]{0:T(1024)S(1)}) all-reduce(f32[4096]{0:T(1024)S(1)} %get-tuple-element.8, f32[4096]{0:T(1024)S(1)} %get-tuple-element.9, ...), channel_id=1, replica_groups=mesh['seq_0'=8,'seq_1'=2,'img_0'=4,'img_1'=2,'fsdp'=2] {'seq_1'}, use_global_device_ids=true, to_apply=%region_8.9 | all-reduce | flops 10240 | bytes 81920 | tf_op jit(solution)/shard_map/psum | solution.py:66
  421.4 14.4 %all-reduce.1 = (f32[4096]{0:T(1024)S(1)}, f32[4096]{0:T(1024)S(1)}, f32[1024]{0:T(1024)S(1)}, f32[1024]{0:T(1024)S(1)}) all-reduce(f32[4096]{0:T(1024)S(1)} %get-tuple-element.24, f32[4096]{0:T(1024)S(1)} %get-tuple-element.25, ...), channel_id=1, replica_groups=mesh['seq_0'=8,'seq_1'=2,'img_0'=4,'img_1'=2,'fsdp'=2] {'img_0'}, use_global_device_ids=true, to_apply=%region_9.10 | all-reduce | flops 10240 | bytes 81920 | tf_op jit(solution)/shard_map/psum | solution.py:66
  435.7 10.3 %all-reduce.3 = (f32[4096]{0:T(1024)S(1)}, f32[4096]{0:T(1024)S(1)}, f32[1024]{0:T(1024)S(1)}, f32[1024]{0:T(1024)S(1)}) all-reduce(f32[4096]{0:T(1024)S(1)} %get-tuple-element.12, f32[4096]{0:T(1024)S(1)} %get-tuple-element.13, ...), channel_id=1, replica_groups=mesh['seq_0'=8,'seq_1'=2,'img_0'=4,'img_1'=2,'fsdp'=2] {'img_1'}, use_global_device_ids=true, to_apply=%region_10.11 | all-reduce | flops 10240 | bytes 81920 | tf_op jit(solution)/shard_map/psum | solution.py:66
  446.0 16.1 %all-reduce.2 = (f32[4096]{0:T(1024)}, f32[4096]{0:T(1024)}, f32[1024]{0:T(1024)}, f32[1024]{0:T(1024)}) all-reduce(f32[4096]{0:T(1024)S(1)} %get-tuple-element.20, f32[4096]{0:T(1024)S(1)} %get-tuple-element.21, f32[1024]{0:T(1024)S(1)} %get-tuple-element.22, ...), channel_id=1, replica_groups=mesh['seq_0'=8,'seq_1'=2,'img_0'=4,'img_1'=2,'fsdp'=2] {'fsdp'}, use_global_device_ids=true, to_apply=%region_11.12 | all-reduce | flops 10240 | bytes 81920 | tf_op jit(solution)/shard_map/psum | solution.py:66
  462.1 0.8 slice.12
  462.9 0.6 reshape.152
  463.6 1.0 slice.13
  464.6 0.7 reshape.153
  (58 shorter events, 0.6 us)
Async XLA Ops:
  7.2 315.1 %copy-start = (bf16[256,2048]{1,0:T(8,128)(2,1)S(1)}, bf16[256,2048]{1,0:T(8,128)(2,1)}, u32[]{:S(2)}) copy-start(bf16[256,2048]{1,0:T(8,128)(2,1)} %param.14) | copy-start | bytes 3145732
  7.2 44.5 %copy-start.13 = (s32[1,2]{1,0:T(1,128)S(1)}, s32[1,2]{1,0:T(1,128)}, u32[]{:S(2)}) copy-start(s32[1,2]{1,0:T(1,128)} %param.16) | copy-start | bytes 28
  7.2 44.8 %copy-start.9 = (s32[1,2304]{1,0:T(1,128)S(1)}, s32[1,2304]{1,0:T(1,128)}, u32[]{:S(2)}) copy-start(s32[1,2304]{1,0:T(1,128)} %param.17) | copy-start | bytes 27652
  7.2 44.4 %all-gather.9.cloned.1.call-start = ((), (), s32[]{:S(2)}) async-start(), calls=%async_computation.5 | async-start | bytes 3145728 | tf_op jit(solution)/shard_map/all_gather | solution.py:36
  7.9 114.2 %all-gather.7.cloned.1.call-start = ((), (), s32[]{:S(2)}) async-start(), calls=%async_computation.4 | async-start | bytes 4866048 | tf_op jit(solution)/shard_map/all_gather | solution.py:128
  8.7 287.3 %all-gather.11.cloned.1.call-start = ((), (), s32[]{:S(2)}) async-start(), calls=%async_computation.6 | async-start | bytes 18874368 | tf_op jit(solution)/shard_map/all_gather | solution.py:36
  128.9 3.8 copy-start.2
  132.6 1.3 copy-start.10
  132.6 1.3 copy-start.11
  138.7 2.1 copy-start.3
  327.8 9.2 %copy-start.8 = (bf16[512,256]{1,0:T(8,128)(2,1)S(1)}, bf16[512,256]{1,0:T(8,128)(2,1)}, u32[]{:S(2)}) copy-start(bf16[512,256]{1,0:T(8,128)(2,1)} %param.12) | copy-start | bytes 786436
  337.9 8.3 %all-to-all-start.1 = ((bf16[2,512,256]{2,1,0:T(8,128)(2,1)}), bf16[2,512,256]{2,1,0:T(8,128)(2,1)S(1)}, u32[]{:S(2)}, u32[]{:S(2)}) async-start(bf16[2,512,256]{2,1,0:T(8,128)(2,1)} %broadcast_in_dim.7), calls=%async_computation.1 | async-start | bytes 1048576 | tf_op jit(solution)/shard_map/all_to_all | solution.py:19
  341.7 4.5 copy-start.12
  341.7 120.4 %reduce-scatter.2.cloned.1.call-start = ((), (), s32[]{:S(2)}) async-start(), calls=%async_computation.3 | async-start | bytes 2949120 | tf_op jit(solution)/shard_map/reduce_scatter | solution.py:56
  341.7 11.2 %slice-start = ((s8[9437184]{0:T(1024)(128)(4,1)}), s8[1048576]{0:T(1024)(128)(4,1)S(1)}, s32[]{:S(2)}) async-start(s8[9437184]{0:T(1024)(128)(4,1)} %bitcast.44), calls=%async_computation.7 | async-start | bytes 2097152
  346.2 6.7 %copy-start.6 = (bf16[2,512,256]{2,1,0:T(8,128)(2,1)}, bf16[2,512,256]{2,1,0:T(8,128)(2,1)S(1)}, u32[]{:S(2)}) copy-start(bf16[2,512,256]{2,1,0:T(8,128)(2,1)S(1)} %all-to-all-done.1) | copy-start | bytes 1572868
  346.2 6.7 %slice-start.1 = ((s8[9437184]{0:T(1024)(128)(4,1)}), s8[4194304]{0:T(1024)(128)(4,1)S(1)}, s32[]{:S(2)}) async-start(s8[9437184]{0:T(1024)(128)(4,1)} %bitcast.44), calls=%async_computation.8 | async-start | bytes 8388608
  346.2 6.7 %slice-start.2 = ((s8[9437184]{0:T(1024)(128)(4,1)}), s8[4194304]{0:T(1024)(128)(4,1)S(1)}, s32[]{:S(2)}) async-start(s8[9437184]{0:T(1024)(128)(4,1)} %bitcast.44), calls=%async_computation.9 | async-start | bytes 8388608
  367.1 9.1 %copy-start.4 = (bf16[1,256,2048]{2,1,0:T(8,128)(2,1)S(1)}, bf16[1,256,2048]{2,1,0:T(8,128)(2,1)}, u32[]{:S(2)}) copy-start(bf16[1,256,2048]{2,1,0:T(8,128)(2,1)} %param.15) | copy-start | bytes 3145732
  367.1 9.6 %copy-start.7 = (bf16[2,512,256]{2,1,0:T(8,128)(2,1)S(1)}, bf16[2,512,256]{2,1,0:T(8,128)(2,1)}, u32[]{:S(2)}) copy-start(bf16[2,512,256]{2,1,0:T(8,128)(2,1)} %copy-done.6) | copy-start | bytes 1572868
  381.8 6.3 %copy-start.5 = (bf16[2304,256]{1,0:T(8,128)(2,1)S(1)}, bf16[2304,256]{1,0:T(8,128)(2,1)}, u32[]{:S(2)}) copy-start(bf16[2304,256]{1,0:T(8,128)(2,1)} %get-tuple-element.30) | copy-start | bytes 3538948
  388.0 77.3 %copy-start.1 = (bf16[256,2048]{1,0:T(8,128)(2,1)S(1)}, bf16[256,2048]{1,0:T(8,128)(2,1)}, u32[]{:S(2)}) copy-start(bf16[256,2048]{1,0:T(8,128)(2,1)} %param.14) | copy-start | bytes 3145732
Sparse Core Ops, SparseCore 0:
  9.8 41.7 all-gather.8
  53.5 68.5 all-gather.6
  123.9 172.0 all-gather.10
  367.2 79.7 reduce-scatter.1
where the time goes:
time: 473 us; the launch traced here: 472 us
  waiting for transfers between devices  268 us (57%)
  blocking collectives  79.1 us (17%)
  local copies, waits for them, and re-layouts  68.7 us (15%)
  matrix products  22.2 us (5%)
  other arithmetic  16 us (3%)
  between operations  14 us (3%)
    all_gather x2, waiting for transfers between devices, whole_of(): nearer = lax.all_gather(array, axes[-1], axis=dim, tiled=True)  196 us
    all_gather x1, waiting for transfers between devices, per_device(): gathered = lax.all_gather(vision_feats[0], SEQ_FSDP, axis=0, tiled=True)  70 us
    psum x5, blocking collectives, one_axis_at_a_time(): array = lax.psum(array, axis)  69.9 us
    gather x1, local copies, waits for them, and re-layouts, per_device(): picked = whole_grad[abs_pos]  26.2 us
    dot_general x4, matrix products, contract(): lax.dot_general(left, right, (((left_dim,), (right_dim,)), ((), ())), pre...  15.2 us
  transfers between devices with their start and end apart: 5, of which 3 were waited for; matrix products, arithmetic and copies ran while one was open for 10% of the time, Pallas kernels for 0%

commit v1 on v0

--- a/solution.py
+++ b/solution.py
@@ -12,6 +12,12 @@
 SEQ_IMG_FSDP = ("seq_0", "seq_1", "img_0", "img_1", "fsdp")
 IMG_FSDP = ("img_0", "img_1", "fsdp")
 SEQ_IMG = ("seq_0", "seq_1", "img_0", "img_1")
+
+
+def summed_here(x, axis):
+    shards = lax.all_gather(x, axis, axis=0, tiled=False)
+    summed = shards.sum(axis=0)
+    return summed
 
 
 def copy_for_each(array, axis):
@@ -63,7 +69,7 @@
 
 def one_axis_at_a_time(array, axes):
     for axis in axes:
-        array = lax.psum(array, axis)
+        array = summed_here(array, axis)
     return array
 
 

time: 473 us -> 600 us (1.27)
  blocking collectives: 79.1 us -> 204 us
    all_gather x0 -> x20, blocking collectives: none -> 195 us  [summed_here(): shards = lax.all_gather(x, axis, axis=0, tiled=False)]
    psum x5 -> x0, blocking collectives: 69.9 us -> none  [one_axis_at_a_time(): array = lax.psum(array, axis)]
  transfers between devices with their start and end apart: 5 -> 5, of which waited for: 3 -> 3; matrix products, arithmetic and copies ran while one was open for 10% -> 8% of each run, Pallas kernels for 0% -> 0%
where the time goes in v1:
time: 600 us
  waiting for transfers between devices  268 us (45%)
  blocking collectives  204 us (34%)
  local copies, waits for them, and re-layouts  68.3 us (11%)
  matrix products  22.2 us (4%)
  other arithmetic  19.1 us (3%)
  between operations  14.1 us (2%)
    all_gather x2, waiting for transfers between devices, whole_of(): nearer = lax.all_gather(array, axes[-1], axis=dim, tiled=True)  196 us
    all_gather x20, blocking collectives, summed_here(): shards = lax.all_gather(x, axis, axis=0, tiled=False)  195 us
    all_gather x1, waiting for transfers between devices, per_device(): gathered = lax.all_gather(vision_feats[0], SEQ_FSDP, axis=0, tiled=True)  70 us
    gather x1, local copies, waits for them, and re-layouts, per_device(): picked = whole_grad[abs_pos]  26.2 us
    dot_general x4, matrix products, contract(): lax.dot_general(left, right, (((left_dim,), (right_dim,)), ((), ())), pre...  15.2 us
  transfers between devices with their start and end apart: 5, of which 3 were waited for; matrix products, arithmetic and copies ran while one was open for 8% of the time, Pallas kernels for 0%

profile of v1, /device:TPU:1, one launch (start us, length us, event | category | flops | bytes accessed | tf_op | source)
XLA Modules:
  0.0 599.6 jit_solution(4410289819049624668)
XLA Ops:
  8.7 42.9 %all-gather.29.cloned.1.call-done = bf16[1,512,2048]{2,1,0:T(8,128)(2,1)} async-done(((bf16[1,256,2048]{2,1,0:T(8,128)(2,1)}), bf16[1,512,2048]{2,1,0:T(8,128)(2,1)}) %all-gather.29.cloned.1.call-update) | async-done | bytes 2097168 | tf_op jit(solution)/shard_map/all_gather | solution.py:42
  52.0 70.0 %all-gather.27.cloned.1.call-done = bf16[1,2304,1024]{2,1,0:T(8,128)(2,1)} async-done(((bf16[1,72,1024]{2,1,0:T(8,128)(2,1)}), bf16[1,2304,1024]{2,1,0:T(8,128)(2,1)}) %all-gather.27.cloned.1.call-update) | async-done | bytes 4718608 | tf_op jit(solution)/shard_map/all_gather | solution.py:134
  122.1 6.8 %copy.20 = bf16[1,2304,1024]{1,2,0:T(8,128)(2,1)} copy(bf16[1,2304,1024]{2,1,0:T(8,128)(2,1)} %all-gather.27.cloned.1.call-done) | data formatting | bytes 9437184 | tf_op jit(solution)/shard_map/all_gather | solution.py:134
  128.9 3.2 convert_reduce_fusion
  132.6 1.3 fusion.3
  133.9 4.8 fusion.1
  138.7 2.1 copy-done.3
  140.9 1.6 constant_dynamic-slice_fusion.2
  142.5 153.5 %all-gather.31.cloned.1.call-done = bf16[1,4096,2048]{2,1,0:T(8,128)(2,1)} async-done(((bf16[1,512,2048]{2,1,0:T(8,128)(2,1)}), bf16[1,4096,2048]{2,1,0:T(8,128)(2,1)}) %all-gather.31.cloned.1.call-update) | async-done | bytes 16777232 | tf_op jit(solution)/shard_map/all_gather | solution.py:42
  296.0 26.2 %gather_fusion = bf16[2304,2048]{1,0:T(8,128)(2,1)} fusion(bf16[4096,2048]{1,0:T(8,128)(2,1)} %bitcast.49, s32[3072]{0:T(1024)S(1)} %pad_clamp_fusion), kind=kCustom, calls=%fused_computation | custom fusion | bytes 18883584 | tf_op jit(solution)/shard_map/gather | solution.py:146
  322.2 5.2 fusion.21
  327.8 9.2 %all_to_all.10 = f32[2,2304,256]{2,1,0:T(8,128)} all-to-all(f32[2,2304,256]{2,1,0:T(8,128)S(1)} %broadcast_in_dim.6), channel_id=1, replica_groups=mesh['seq_0'=8,'seq_1'=2,'img_0'=4,'img_1'=2,'fsdp'=2] {'fsdp'}, dimensions={0} | all-to-all | bytes 9437184 | tf_op jit(solution)/shard_map/all_to_all | solution.py:25
  337.0 0.8 broadcast_in_dim.7
  337.8 3.8 all-to-all-start.1
  341.7 4.5 reduce_sum.246
  346.2 6.7 %fusion.9 = (bf16[2304,256]{1,0:T(8,128)(2,1)}, f32[2304,256]{1,0:T(8,128)S(1)}) fusion(f32[2304,256]{1,0:T(8,128)} %reduce_sum.246, f32[256]{0:T(256)S(1)} %copy-done.12, bf16[2304,1024]{0,1:T(8,128)(2,1)} %copy-done.3, bf16[1024,256]{1,0:T(8,128)(2,1)S(1)} %bitcast.56), kind=kOutput, calls=%fused_computation.18 | convolution fusion | flops 1214447616 | bytes 11142144 | tf_op jit(solution)/shard_map/dot_general | solution.py:141
  352.9 4.0 fusion.11
  356.9 2.0 reshape_reshape.7
  358.9 2.8 fusion.22
  361.8 1.7 pad_maximum_fusion
  363.5 3.6 reshape.149
  367.1 9.0 %scatter_custom_fusion = f32[4096]{0:T(1024)S(1)} fusion(s32[2304]{0:T(1024)S(1)} %fusion.17, f32[2304]{0:T(1024)S(1)} %broadcast.83, f32[]{:T(128)} %constant.22.clone.1), kind=kCustom, calls=%fused_computation.40 | custom fusion | bytes 16388 | tf_op jit(solution)/shard_map/scatter | solution.py:122
  376.5 19.8 %all-gather.20 = f32[8,1,4096]{2,1,0:T(1,128)S(1)} all-gather(f32[1,1,4096]{2,1,0:T(1,128)S(1)} %fusion.10), channel_id=1, replica_groups=mesh['seq_0'=8,'seq_1'=2,'img_0'=4,'img_1'=2,'fsdp'=2] {'seq_0'}, dimensions={0}, use_global_device_ids=true | all-gather | bytes 147456 | tf_op jit(solution)/shard_map/all_gather | solution.py:18
  396.4 3.7 all-gather.7
  400.2 9.6 %all-gather.8 = f32[16384]{0:T(1024)S(1)} all-gather(f32[4096]{0:T(1024)S(1)} %reduce_sum.254), channel_id=10, replica_groups=mesh['seq_0'=8,'seq_1'=2,'img_0'=4,'img_1'=2,'fsdp'=2] {'img_0'}, dimensions={0}, use_global_device_ids=true | all-gather | bytes 81920 | tf_op jit(solution)/shard_map/all_gather | solution.py:18
  409.8 4.8 all-gather.9
  414.7 11.0 %all-gather.10 = f32[8192]{0:T(1024)S(1)} all-gather(f32[4096]{0:T(1024)S(1)} %reduce_sum.256), channel_id=12, replica_groups=mesh['seq_0'=8,'seq_1'=2,'img_0'=4,'img_1'=2,'fsdp'=2] {'fsdp'}, dimensions={0}, use_global_device_ids=true | all-gather | bytes 49152 | tf_op jit(solution)/shard_map/all_gather | solution.py:18
  426.3 4.8 constant_dynamic-slice_fusion
  431.2 6.3 %copy.21 = f32[2304,512]{1,0:T(8,128)} copy(f32[2304,512]{0,1:T(8,128)} %bitcast.53) | data formatting | bytes 9437184 | tf_op jit(solution)/shard_map/reshape | solution.py:93
  437.7 19.4 %all-gather.19 = f32[8,1,4096]{2,1,0:T(1,128)S(1)} all-gather(f32[1,1,4096]{2,1,0:T(1,128)S(1)} %constant_dynamic-update-slice_fusion), channel_id=1, replica_groups=mesh['seq_0'=8,'seq_1'=2,'img_0'=4,'img_1'=2,'fsdp'=2] {'seq_0'}, dimensions={0}, use_global_device_ids=true | all-gather | bytes 147456 | tf_op jit(solution)/shard_map/all_gather | solution.py:18
  457.2 3.3 all-gather.3
  460.5 9.0 %all-gather.4 = f32[16384]{0:T(1024)S(1)} all-gather(f32[4096]{0:T(1024)S(1)} %reduce_sum.249), channel_id=6, replica_groups=mesh['seq_0'=8,'seq_1'=2,'img_0'=4,'img_1'=2,'fsdp'=2] {'img_0'}, dimensions={0}, use_global_device_ids=true | all-gather | bytes 81920 | tf_op jit(solution)/shard_map/all_gather | solution.py:18
  469.5 4.8 all-gather.5
  474.4 12.1 %all-gather.6 = f32[8192]{0:T(1024)S(1)} all-gather(f32[4096]{0:T(1024)S(1)} %reduce_sum.251), channel_id=8, replica_groups=mesh['seq_0'=8,'seq_1'=2,'img_0'=4,'img_1'=2,'fsdp'=2] {'fsdp'}, dimensions={0}, use_global_device_ids=true | all-gather | bytes 49152 | tf_op jit(solution)/shard_map/all_gather | solution.py:18
  486.6 3.2 fusion.20
  490.0 18.3 %all-gather.21 = f32[8,1,1024]{2,1,0:T(1,128)S(1)} all-gather(f32[1,1,1024]{2,1,0:T(1,128)S(1)} %reshape.198), channel_id=1, replica_groups=mesh['seq_0'=8,'seq_1'=2,'img_0'=4,'img_1'=2,'fsdp'=2] {'seq_0'}, dimensions={0}, use_global_device_ids=true | all-gather | bytes 36864 | tf_op jit(solution)/shard_map/all_gather | solution.py:18
  508.3 3.2 all-gather.11
  511.6 9.1 %all-gather.12 = f32[4096]{0:T(1024)S(1)} all-gather(f32[1024]{0:T(1024)S(1)} %reduce_sum.260), channel_id=14, replica_groups=mesh['seq_0'=8,'seq_1'=2,'img_0'=4,'img_1'=2,'fsdp'=2] {'img_0'}, dimensions={0}, use_global_device_ids=true | all-gather | bytes 20480 | tf_op jit(solution)/shard_map/all_gather | solution.py:18
  520.7 4.7 all-gather.13
  525.5 13.4 %all-gather.14 = f32[2048]{0:T(1024)S(1)} all-gather(f32[1024]{0:T(1024)S(1)} %reduce_sum.262), channel_id=16, replica_groups=mesh['seq_0'=8,'seq_1'=2,'img_0'=4,'img_1'=2,'fsdp'=2] {'fsdp'}, dimensions={0}, use_global_device_ids=true | all-gather | bytes 12288 | tf_op jit(solution)/shard_map/all_gather | solution.py:18
  539.1 18.3 %all-gather.22 = f32[8,1,1024]{2,1,0:T(1,128)S(1)} all-gather(f32[1,1,1024]{2,1,0:T(1,128)S(1)} %reshape.200), channel_id=1, replica_groups=mesh['seq_0'=8,'seq_1'=2,'img_0'=4,'img_1'=2,'fsdp'=2] {'seq_0'}, dimensions={0}, use_global_device_ids=true | all-gather | bytes 36864 | tf_op jit(solution)/shard_map/all_gather | solution.py:18
  557.4 3.2 all-gather.15
  560.7 9.1 %all-gather.16 = f32[4096]{0:T(1024)S(1)} all-gather(f32[1024]{0:T(1024)S(1)} %reduce_sum.266), channel_id=18, replica_groups=mesh['seq_0'=8,'seq_1'=2,'img_0'=4,'img_1'=2,'fsdp'=2] {'img_0'}, dimensions={0}, use_global_device_ids=true | all-gather | bytes 20480 | tf_op jit(solution)/shard_map/all_gather | solution.py:18
  569.8 4.7 all-gather.17
  574.6 13.4 %all-gather.18 = f32[2048]{0:T(1024)S(1)} all-gather(f32[1024]{0:T(1024)S(1)} %reduce_sum.268), channel_id=20, replica_groups=mesh['seq_0'=8,'seq_1'=2,'img_0'=4,'img_1'=2,'fsdp'=2] {'fsdp'}, dimensions={0}, use_global_device_ids=true | all-gather | bytes 12288 | tf_op jit(solution)/shard_map/all_gather | solution.py:18
  589.8 0.8 slice.12
  591.3 1.0 slice.13
  592.3 0.7 reshape.151
  (108 shorter events, 7.9 us)
Async XLA Ops:
  7.2 315.1 %copy-start = (bf16[256,2048]{1,0:T(8,128)(2,1)S(1)}, bf16[256,2048]{1,0:T(8,128)(2,1)}, u32[]{:S(2)}) copy-start(bf16[256,2048]{1,0:T(8,128)(2,1)} %param.14) | copy-start | bytes 3145732
  7.2 44.5 %copy-start.13 = (s32[1,2]{1,0:T(1,128)S(1)}, s32[1,2]{1,0:T(1,128)}, u32[]{:S(2)}) copy-start(s32[1,2]{1,0:T(1,128)} %param.16) | copy-start | bytes 28
  7.2 44.8 %copy-start.9 = (s32[1,2304]{1,0:T(1,128)S(1)}, s32[1,2304]{1,0:T(1,128)}, u32[]{:S(2)}) copy-start(s32[1,2304]{1,0:T(1,128)} %param.17) | copy-start | bytes 27652
  7.2 44.4 %all-gather.29.cloned.1.call-start = ((), (), s32[]{:S(2)}) async-start(), calls=%async_computation.5 | async-start | bytes 3145728 | tf_op jit(solution)/shard_map/all_gather | solution.py:42
  7.9 114.2 %all-gather.27.cloned.1.call-start = ((), (), s32[]{:S(2)}) async-start(), calls=%async_computation.4 | async-start | bytes 4866048 | tf_op jit(solution)/shard_map/all_gather | solution.py:134
  8.7 287.3 %all-gather.31.cloned.1.call-start = ((), (), s32[]{:S(2)}) async-start(), calls=%async_computation.6 | async-start | bytes 18874368 | tf_op jit(solution)/shard_map/all_gather | solution.py:42
  128.9 3.8 copy-start.2
  132.6 1.3 copy-start.10
  132.6 1.3 copy-start.11
  138.7 2.1 copy-start.3
  327.8 9.2 %copy-start.8 = (bf16[512,256]{1,0:T(8,128)(2,1)S(1)}, bf16[512,256]{1,0:T(8,128)(2,1)}, u32[]{:S(2)}) copy-start(bf16[512,256]{1,0:T(8,128)(2,1)} %param.12) | copy-start | bytes 786436
  337.8 8.3 %all-to-all-start.1 = ((bf16[2,512,256]{2,1,0:T(8,128)(2,1)}), bf16[2,512,256]{2,1,0:T(8,128)(2,1)S(1)}, u32[]{:S(2)}, u32[]{:S(2)}) async-start(bf16[2,512,256]{2,1,0:T(8,128)(2,1)} %broadcast_in_dim.7), calls=%async_computation.1 | async-start | bytes 1048576 | tf_op jit(solution)/shard_map/all_to_all | solution.py:25
  341.7 4.5 copy-start.12
  341.7 248.1 %reduce-scatter.2.cloned.1.call-start = ((), (), s32[]{:S(2)}) async-start(), calls=%async_computation.3 | async-start | bytes 2949120 | tf_op jit(solution)/shard_map/reduce_scatter | solution.py:62
  341.7 11.2 %slice-start = ((s8[9437184]{0:T(1024)(128)(4,1)}), s8[1048576]{0:T(1024)(128)(4,1)S(1)}, s32[]{:S(2)}) async-start(s8[9437184]{0:T(1024)(128)(4,1)} %bitcast.50), calls=%async_computation.7 | async-start | bytes 2097152
  346.2 6.7 %copy-start.6 = (bf16[2,512,256]{2,1,0:T(8,128)(2,1)}, bf16[2,512,256]{2,1,0:T(8,128)(2,1)S(1)}, u32[]{:S(2)}) copy-start(bf16[2,512,256]{2,1,0:T(8,128)(2,1)S(1)} %all-to-all-done.1) | copy-start | bytes 1572868
  346.2 6.7 %slice-start.1 = ((s8[9437184]{0:T(1024)(128)(4,1)}), s8[4194304]{0:T(1024)(128)(4,1)S(1)}, s32[]{:S(2)}) async-start(s8[9437184]{0:T(1024)(128)(4,1)} %bitcast.50), calls=%async_computation.8 | async-start | bytes 8388608
  346.2 6.7 %slice-start.2 = ((s8[9437184]{0:T(1024)(128)(4,1)}), s8[4194304]{0:T(1024)(128)(4,1)S(1)}, s32[]{:S(2)}) async-start(s8[9437184]{0:T(1024)(128)(4,1)} %bitcast.50), calls=%async_computation.9 | async-start | bytes 8388608
  367.1 9.2 %copy-start.4 = (bf16[1,256,2048]{2,1,0:T(8,128)(2,1)S(1)}, bf16[1,256,2048]{2,1,0:T(8,128)(2,1)}, u32[]{:S(2)}) copy-start(bf16[1,256,2048]{2,1,0:T(8,128)(2,1)} %param.15) | copy-start | bytes 3145732
  367.1 59.2 %copy-start.7 = (bf16[2,512,256]{2,1,0:T(8,128)(2,1)S(1)}, bf16[2,512,256]{2,1,0:T(8,128)(2,1)}, u32[]{:S(2)}) copy-start(bf16[2,512,256]{2,1,0:T(8,128)(2,1)} %copy-done.6) | copy-start | bytes 1572868
  431.2 6.3 %copy-start.5 = (bf16[2304,256]{1,0:T(8,128)(2,1)S(1)}, bf16[2304,256]{1,0:T(8,128)(2,1)}, u32[]{:S(2)}) copy-start(bf16[2304,256]{1,0:T(8,128)(2,1)} %get-tuple-element.10) | copy-start | bytes 3538948
  486.5 106.5 %copy-start.1 = (bf16[256,2048]{1,0:T(8,128)(2,1)S(1)}, bf16[256,2048]{1,0:T(8,128)(2,1)}, u32[]{:S(2)}) copy-start(bf16[256,2048]{1,0:T(8,128)(2,1)} %param.14) | copy-start | bytes 3145732
Sparse Core Ops, SparseCore 0:
  9.8 41.7 all-gather.28
  53.5 68.5 all-gather.26
  123.9 172.0 all-gather.30
  367.2 79.6 reduce-scatter.1
